TPU v7x, 32 devices: a whole 2x2x4 slice. The times are simulated.
32 devices in a mesh: band: 8 (over y, x, core), grid: 4 (over z).
Axes of the slice: x: 2, y: 2, z: 4, core: 2. Of those that a mesh axis runs over, the one named last changes fastest.
Arguments:
- wave: bfloat16 [4096, 10240], P('band', 'grid'), may hold values from -6 to 6
- ritz: bfloat16 [4096, 4096], P('band', 'grid'), may hold values from -0.125 to 0.125
- occupation: float32 [4096], P('band'), may hold values from 0 to 2
Outputs:
- rotated: bfloat16 [4096, 10240], P('band', 'grid')
- density: float32 [10240], P('grid')
All inputs are finite; a program needn't handle non-finite values.
Results may differ from a plain program's by a relative error of at most 0.0017.
Values may be sent and summed in bfloat16 or wider, within the bound.
A program may use at most 128 MiB of HBM per device.

v0:
```python
import jax
import jax.numpy as jnp
from jax import lax
from jax.sharding import PartitionSpec as P

NB = 4096


def per_device(wave, ritz, occupation):
    ritz_rows = lax.all_gather(ritz, "grid", axis=1, tiled=True)
    ritz_cols = lax.all_to_all(ritz_rows, "band", split_axis=1, concat_axis=0, tiled=True)
    summed = lax.dot_general(
        ritz_cols,
        lax.all_gather(wave, "band", axis=0, tiled=True),
        (((0,), (0,)), ((), ())),
        preferred_element_type=jnp.float32,
    )
    rotated = summed.astype(jnp.bfloat16)
    values = rotated.astype(jnp.float32)
    partial_terms = jnp.sum(occupation[:, None] * values * values, axis=0)
    density = lax.psum(partial_terms, "band") / NB
    return (rotated, density)


def solution(mesh):
    return jax.shard_map(
        per_device,
        mesh=mesh,
        in_specs=(P("band", "grid"), P("band", "grid"), P("band")),
        out_specs=(P("band", "grid"), P("grid")),
        check_vma=False,
    )
```

profile of v0, /device:TPU:0, one launch (start us, length us, event | category | flops | bytes accessed | tf_op | source)
XLA Modules:
  0.0 287.0 jit_solution(8882897534836297578)
XLA Ops:
  7.2 0.0 all-gather.3.cloned.1.call-start
  7.2 2.3 copy.5
  9.5 0.0 all-gather.3.cloned.1.call-update
  9.5 0.0 all-gather.5.cloned.1.call-start
  9.6 0.7 all-gather.5.cloned.1.call-update
  10.3 83.3 %all-gather.3.cloned.1.call-done = bf16[512,4096]{0,1:T(8,128)(2,1)} async-done(((bf16[512,1024]{0,1:T(8,128)(2,1)}), bf16[512,4096]{0,1:T(8,128)(2,1)}) %all-gather.3.cloned.1.call-update) | async-done | bytes 4194320 | tf_op jit(solution)/shard_map/all_gather | solution.py:10
  93.6 81.7 %all_to_all.19 = bf16[512,8,512]{0,2,1:T(8,128)(2,1)} all-to-all(bf16[512,8,512]{0,2,1:T(8,128)(2,1)} %bitcast.6), channel_id=1, replica_groups=mesh['band'=8,'grid'=4] {'band'}, dimensions={1} | all-to-all | bytes 8388608 | tf_op jit(solution)/shard_map/all_to_all | solution.py:11
  175.3 0.0 copy-start
  175.3 6.8 %copy.6 = bf16[8,512,512]{2,1,0:T(8,128)(2,1)} copy(bf16[8,512,512]{1,2,0:T(8,128)(2,1)} %bitcast.5) | data formatting | bytes 8388608 | tf_op jit(solution)/shard_map/all_to_all | solution.py:11
  182.1 56.3 %all-gather.5.cloned.1.call-done = bf16[4096,2560]{1,0:T(8,128)(2,1)} async-done(((bf16[512,2560]{1,0:T(8,128)(2,1)}), bf16[4096,2560]{1,0:T(8,128)(2,1)}) %all-gather.5.cloned.1.call-update) | async-done | bytes 20971536 | tf_op jit(solution)/shard_map/all_gather | solution.py:14
  238.4 0.0 copy-done
  238.4 17.7 %fusion = (f32[2560]{0:T(1024)S(1)}, bf16[512,2560]{1,0:T(8,128)(2,1)}) fusion(f32[512]{0:T(512)S(1)} %copy-done, bf16[4096,512]{1,0:T(8,128)(2,1)} %bitcast.7, bf16[4096,2560]{1,0:T(8,128)(2,1)} %all-gather.5.cloned.1.call-done), kind=kOutput, calls=%fused_computation.1 | convolution fusion | flops 10743969792 | bytes 27799552 | tf_op jit(solution)/shard_map/dot_general | solution.py:12
  256.1 23.5 %psum.7 = f32[2560]{0:T(1024)S(1)} all-reduce(f32[2560]{0:T(1024)S(1)} %get-tuple-element.2), channel_id=1, replica_groups=mesh['band'=8,'grid'=4] {'band'}, use_global_device_ids=true, to_apply=%region_1.0 | all-reduce | flops 2560 | bytes 20480 | tf_op jit(solution)/shard_map/psum | solution.py:21
  279.5 0.6 broadcast_multiply_fusion
Async XLA Ops:
  7.2 86.4 %all-gather.3.cloned.1.call-start = ((), (), s32[]{:S(2)}) async-start(), calls=%async_computation.1 | async-start | bytes 5242880 | tf_op jit(solution)/shard_map/all_gather | solution.py:10
  9.5 228.9 %all-gather.5.cloned.1.call-start = ((), (), s32[]{:S(2)}) async-start(), calls=%async_computation.2 | async-start | bytes 23592960 | tf_op jit(solution)/shard_map/all_gather | solution.py:14
  175.3 63.1 %copy-start = (f32[512]{0:T(512)S(1)}, f32[512]{0:T(512)}, u32[]{:S(2)}) copy-start(f32[512]{0:T(512)} %param.5) | copy-start | bytes 6148
Sparse Core Ops, SparseCore 0:
  10.1 83.4 all-gather.2
  95.5 142.8 all-gather.4
where the time goes:
time: 287 us
  waiting for transfers between devices  140 us (49%)
  blocking collectives  105 us (37%)
  matrix products  17.7 us (6%)
  between operations  14 us (5%)
  local copies, waits for them, and re-layouts  9.09 us (3%)
    all_gather x1, waiting for transfers between devices, per_device(): ritz_rows = lax.all_gather(ritz, 'grid', axis=1, tiled=True)  83.3 us
    all_to_all x1, blocking collectives, per_device(): lax.all_to_all(ritz_rows, 'band', split_axis=1, concat_axis=0, tiled=True)  81.7 us
    all_gather x1, waiting for transfers between devices, per_device(): lax.all_gather(wave, 'band', axis=0, tiled=True)  56.3 us
    psum x1, blocking collectives, per_device(): density = lax.psum(partial_terms, 'band') / NB  23.5 us
    dot_general x1, matrix products, per_device(): lax.dot_general(ritz_cols, lax.all_gather(wave, 'band', axis=0, tiled=Tru...  17.7 us
    all_to_all x1, local copies, waits for them, and re-layouts, per_device(): lax.all_to_all(ritz_rows, 'band', split_axis=1, concat_axis=0, tiled=True)  6.81 us
  transfers between devices with their start and end apart: 2, of which 2 were waited for; matrix products, arithmetic and copies ran while one was open for 2% of the time, Pallas kernels for 0%

commit v1 on v0

--- a/solution.py
+++ b/solution.py
@@ -7,7 +7,12 @@
 
 
 def per_device(wave, ritz, occupation):
-    ritz_rows = lax.all_gather(ritz, "grid", axis=1, tiled=True)
+    ring = [ritz]
+    for hop in range(3):
+        ring.append(lax.ppermute(ring[-1], "grid", [(dev, (dev + 1) % 4) for dev in range(4)]))
+    ritz_rows = jnp.roll(
+        jnp.concatenate(ring[::-1], axis=1), (lax.axis_index("grid") + 1) * ring[0].shape[1], axis=1
+    )
     ritz_cols = lax.all_to_all(ritz_rows, "band", split_axis=1, concat_axis=0, tiled=True)
     summed = lax.dot_general(
         ritz_cols,

time: 287 us -> 218 us (0.76)
  waiting for transfers between devices: 140 us -> 77.4 us
  blocking collectives: 105 us -> 93 us
  starting transfers between devices: 0.08 us -> 3.15 us
    all_gather x1 -> x0, waiting for transfers between devices: 83.3 us -> none  [per_device(): ritz_rows = lax.all_gather(ritz, 'grid', axis=1, tiled=True)]
    ppermute x0 -> x3, waiting for transfers between devices: none -> 76.7 us  [per_device(): lax.ppermute(ring[-1], 'grid', [(dev, (dev + 1) % 4) for dev in range(4)])]
    all_gather x1, waiting for transfers between devices: 56.3 us -> 0.01 us  [per_device(): lax.all_gather(wave, 'band', axis=0, tiled=True)]
    all_to_all x1, blocking collectives: 81.7 us -> 70.7 us  [per_device(): lax.all_to_all(ritz_rows, 'band', split_axis=1, concat_axis=0, tiled=True)]
    ppermute x0 -> x3, starting transfers between devices: none -> 3.11 us  [per_device(): lax.ppermute(ring[-1], 'grid', [(dev, (dev + 1) % 4) for dev in range(4)])]
  transfers between devices with their start and end apart: 2 -> 4, of which waited for: 2 -> 3; matrix products, arithmetic and copies ran while one was open for 2% -> 5% of each run, Pallas kernels for 0% -> 0%
where the time goes in v1:
time: 218 us; the launch traced here: 217 us
  blocking collectives  93 us (43%)
  waiting for transfers between devices  77.4 us (36%)
  matrix products  17.7 us (8%)
  between operations  14.1 us (6%)
  local copies, waits for them, and re-layouts  11.3 us (5%)
  starting transfers between devices  3.15 us (1%)
    ppermute x3, waiting for transfers between devices, per_device(): lax.ppermute(ring[-1], 'grid', [(dev, (dev + 1) % 4) for dev in range(4)])  76.7 us
    all_to_all x1, blocking collectives, per_device(): lax.all_to_all(ritz_rows, 'band', split_axis=1, concat_axis=0, tiled=True)  70.7 us
    psum x1, blocking collectives, per_device(): density = lax.psum(partial_terms, 'band') / NB  22.3 us
    dot_general x1, matrix products, per_device(): lax.dot_general(ritz_cols, lax.all_gather(wave, 'band', axis=0, tiled=Tru...  17.7 us
    all_to_all x1, local copies, waits for them, and re-layouts, per_device(): lax.all_to_all(ritz_rows, 'band', split_axis=1, concat_axis=0, tiled=True)  6.5 us
    unnamed x10, local copies, waits for them, and re-layouts  4.44 us
  transfers between devices with their start and end apart: 4, of which 3 were waited for; matrix products, arithmetic and copies ran while one was open for 5% of the time, Pallas kernels for 0%

profile of v1, /device:TPU:0, one launch (start us, length us, event | category | flops | bytes accessed | tf_op | source)
XLA Modules:
  0.0 217.2 jit_solution(4942098505358791003)
XLA Ops:
  7.2 0.0 all-gather.2.cloned.1.call-start
  7.2 0.7 all-gather.2.cloned.1.call-update
  7.9 1.5 copy.5
  9.4 3.1 %collective-permute-start = (bf16[512,1024]{0,1:T(8,128)(2,1)S(1)}, bf16[512,1024]{0,1:T(8,128)(2,1)S(1)}, u32[]{:S(2)}, u32[]{:S(2)}) collective-permute-start(bf16[512,1024]{0,1:T(8,128)(2,1)S(1)} %copy.5), channel_id=1, source_target_pairs={{0,1},{1,2},{2,3},{3,0},{4,5},{5,6},{6,7},{7,4},{8,9},{9,10},{10,1... | collective-permute-start | bytes 3145736 | tf_op jit(solution)/shard_map/ppermute | solution.py:12
  12.5 25.2 %collective-permute-done = bf16[512,1024]{0,1:T(8,128)(2,1)S(1)} collective-permute-done((bf16[512,1024]{0,1:T(8,128)(2,1)S(1)}, bf16[512,1024]{0,1:T(8,128)(2,1)S(1)}, u32[]{:S(2)}, u32[]{:S(2)}) %collective-permute-start) | collective-permute-done | bytes 1048608 | tf_op jit(solution)/shard_map/ppermute | solution.py:12
  37.7 0.0 collective-permute-start.1
  37.7 26.1 %collective-permute-done.1 = bf16[512,1024]{0,1:T(8,128)(2,1)S(1)} collective-permute-done((bf16[512,1024]{0,1:T(8,128)(2,1)S(1)}, bf16[512,1024]{0,1:T(8,128)(2,1)S(1)}, u32[]{:S(2)}, u32[]{:S(2)}) %collective-permute-start.1) | collective-permute-done | bytes 1048608 | tf_op jit(solution)/shard_map/ppermute | solution.py:12
  63.8 0.0 collective-permute-start.2
  63.8 25.4 %collective-permute-done.2 = bf16[512,1024]{0,1:T(8,128)(2,1)} collective-permute-done((bf16[512,1024]{0,1:T(8,128)(2,1)S(1)}, bf16[512,1024]{0,1:T(8,128)(2,1)}, u32[]{:S(2)}, u32[]{:S(2)}) %collective-permute-start.2) | collective-permute-done | bytes 1048608 | tf_op jit(solution)/shard_map/ppermute | solution.py:12
  89.2 1.3 constant_dynamic-update-slice_fusion.7
  90.5 0.1 constant_dynamic-update-slice_fusion.6
  90.6 0.1 constant_dynamic-update-slice_fusion.5
  90.6 0.1 constant_dynamic-update-slice_fusion.4
  90.7 1.3 constant_dynamic-update-slice_fusion.3
  92.0 0.1 constant_dynamic-update-slice_fusion.2
  92.1 0.1 constant_dynamic-update-slice_fusion.1
  92.2 0.1 constant_dynamic-update-slice_fusion
  92.2 0.3 constant_dynamic-slice_fusion
  92.5 0.0 copy-start
  92.5 70.7 %all_to_all.19 = bf16[512,8,512]{0,2,1:T(8,128)(2,1)} all-to-all(bf16[512,8,512]{0,2,1:T(8,128)(2,1)S(1)} %bitcast.5), channel_id=1, replica_groups=mesh['band'=8,'grid'=4] {'band'}, dimensions={1} | all-to-all | bytes 8388608 | tf_op jit(solution)/shard_map/all_to_all | solution.py:16
  163.2 6.5 %copy.8 = bf16[8,512,512]{2,1,0:T(8,128)(2,1)} copy(bf16[8,512,512]{1,2,0:T(8,128)(2,1)} %bitcast.6) | data formatting | bytes 8388608 | tf_op jit(solution)/shard_map/all_to_all | solution.py:16
  169.7 0.0 all-gather.2.cloned.1.call-done
  169.7 0.0 copy-done
  169.7 17.7 %fusion = (f32[2560]{0:T(1024)S(1)}, bf16[512,2560]{1,0:T(8,128)(2,1)}) fusion(f32[512]{0:T(512)S(1)} %copy-done, bf16[4096,512]{1,0:T(8,128)(2,1)} %bitcast.7, bf16[4096,2560]{1,0:T(8,128)(2,1)} %all-gather.2.cloned.1.call-done), kind=kOutput, calls=%fused_computation.1 | convolution fusion | flops 10743969792 | bytes 27799552 | tf_op jit(solution)/shard_map/dot_general | solution.py:17
  187.4 22.3 %psum.7 = f32[2560]{0:T(1024)S(1)} all-reduce(f32[2560]{0:T(1024)S(1)} %get-tuple-element.2), channel_id=1, replica_groups=mesh['band'=8,'grid'=4] {'band'}, use_global_device_ids=true, to_apply=%region_1.2 | all-reduce | flops 2560 | bytes 20480 | tf_op jit(solution)/shard_map/psum | solution.py:26
  209.8 0.6 broadcast_multiply_fusion
Async XLA Ops:
  7.2 162.6 %all-gather.2.cloned.1.call-start = ((), (), s32[]{:S(2)}) async-start(), calls=%async_computation.1 | async-start | bytes 23592960 | tf_op jit(solution)/shard_map/all_gather | solution.py:19
  9.4 28.3 %collective-permute-start = (bf16[512,1024]{0,1:T(8,128)(2,1)S(1)}, bf16[512,1024]{0,1:T(8,128)(2,1)S(1)}, u32[]{:S(2)}, u32[]{:S(2)}) collective-permute-start(bf16[512,1024]{0,1:T(8,128)(2,1)S(1)} %copy.5), channel_id=1, source_target_pairs={{0,1},{1,2},{2,3},{3,0},{4,5},{5,6},{6,7},{7,4},{8,9},{9,10},{10,1... | collective-permute-start | bytes 3145736 | tf_op jit(solution)/shard_map/ppermute | solution.py:12
  37.7 26.1 %collective-permute-start.1 = (bf16[512,1024]{0,1:T(8,128)(2,1)S(1)}, bf16[512,1024]{0,1:T(8,128)(2,1)S(1)}, u32[]{:S(2)}, u32[]{:S(2)}) collective-permute-start(bf16[512,1024]{0,1:T(8,128)(2,1)S(1)} %collective-permute-done), channel_id=1, source_target_pairs={{0,1},{1,2},{2,3},{3,0},{4,5},{5,6},{6,7},{7,4},{8,9},{9,10},{10,1... | collective-permute-start | bytes 3145736 | tf_op jit(solution)/shard_map/ppermute | solution.py:12
  63.8 25.4 %collective-permute-start.2 = (bf16[512,1024]{0,1:T(8,128)(2,1)S(1)}, bf16[512,1024]{0,1:T(8,128)(2,1)}, u32[]{:S(2)}, u32[]{:S(2)}) collective-permute-start(bf16[512,1024]{0,1:T(8,128)(2,1)S(1)} %collective-permute-done.1), channel_id=1, source_target_pairs={{0,1},{1,2},{2,3},{3,0},{4,5},{5,6},{6,7},{7,4},{8,9},{9,10},{10,1... | collective-permute-start | bytes 3145736 | tf_op jit(solution)/shard_map/ppermute | solution.py:12
  92.5 77.2 %copy-start = (f32[512]{0:T(512)S(1)}, f32[512]{0:T(512)}, u32[]{:S(2)}) copy-start(f32[512]{0:T(512)} %param.5) | copy-start | bytes 6148
Sparse Core Ops, SparseCore 0:
  9.9 145.3 all-gather.1

commit v2 on v0

--- a/solution.py
+++ b/solution.py
@@ -18,7 +18,7 @@
     rotated = summed.astype(jnp.bfloat16)
     values = rotated.astype(jnp.float32)
     partial_terms = jnp.sum(occupation[:, None] * values * values, axis=0)
-    density = lax.psum(partial_terms, "band") / NB
+    density = jnp.sum(lax.all_gather(partial_terms, "band"), axis=0) / NB
     return (rotated, density)
 
 

time: 287 us -> 273 us (0.951)
  blocking collectives: 105 us -> 90.9 us
    psum x1 -> x0, blocking collectives: 23.5 us -> none  [per_device(): density = lax.psum(partial_terms, 'band') / NB]
    all_gather x0 -> x1, blocking collectives: none -> 9.24 us  [per_device(): density = jnp.sum(lax.all_gather(partial_terms, 'band'), axis=0) / NB]
where the time goes in v2:
time: 273 us
  waiting for transfers between devices  140 us (51%)
  blocking collectives  90.9 us (33%)
  matrix products  17.7 us (6%)
  between operations  14 us (5%)
  local copies, waits for them, and re-layouts  9.1 us (3%)
    all_gather x1, waiting for transfers between devices, per_device(): ritz_rows = lax.all_gather(ritz, 'grid', axis=1, tiled=True)  83.3 us
    all_to_all x1, blocking collectives, per_device(): lax.all_to_all(ritz_rows, 'band', split_axis=1, concat_axis=0, tiled=True)  81.7 us
    all_gather x1, waiting for transfers between devices, per_device(): lax.all_gather(wave, 'band', axis=0, tiled=True)  56.3 us
    dot_general x1, matrix products, per_device(): lax.dot_general(ritz_cols, lax.all_gather(wave, 'band', axis=0, tiled=Tru...  17.7 us
    all_gather x1, blocking collectives, per_device(): density = jnp.sum(lax.all_gather(partial_terms, 'band'), axis=0) / NB  9.24 us
    all_to_all x1, local copies, waits for them, and re-layouts, per_device(): lax.all_to_all(ritz_rows, 'band', split_axis=1, concat_axis=0, tiled=True)  6.81 us
  transfers between devices with their start and end apart: 2, of which 2 were waited for; matrix products, arithmetic and copies ran while one was open for 2% of the time, Pallas kernels for 0%

profile of v2, /device:TPU:0, one launch (start us, length us, event | category | flops | bytes accessed | tf_op | source)
XLA Modules:
  0.0 272.8 jit_solution(13163691572105657755)
XLA Ops:
  7.2 0.0 all-gather.5.cloned.1.call-start
  7.2 2.3 copy.7
  9.5 0.0 all-gather.5.cloned.1.call-update
  9.5 0.0 all-gather.7.cloned.1.call-start
  9.6 0.7 all-gather.7.cloned.1.call-update
  10.3 83.3 %all-gather.5.cloned.1.call-done = bf16[512,4096]{0,1:T(8,128)(2,1)} async-done(((bf16[512,1024]{0,1:T(8,128)(2,1)}), bf16[512,4096]{0,1:T(8,128)(2,1)}) %all-gather.5.cloned.1.call-update) | async-done | bytes 4194320 | tf_op jit(solution)/shard_map/all_gather | solution.py:10
  93.6 81.7 %all_to_all.19 = bf16[512,8,512]{0,2,1:T(8,128)(2,1)} all-to-all(bf16[512,8,512]{0,2,1:T(8,128)(2,1)} %bitcast.6), channel_id=1, replica_groups=mesh['band'=8,'grid'=4] {'band'}, dimensions={1} | all-to-all | bytes 8388608 | tf_op jit(solution)/shard_map/all_to_all | solution.py:11
  175.3 0.0 copy-start
  175.3 6.8 %copy.8 = bf16[8,512,512]{2,1,0:T(8,128)(2,1)} copy(bf16[8,512,512]{1,2,0:T(8,128)(2,1)} %bitcast.5) | data formatting | bytes 8388608 | tf_op jit(solution)/shard_map/all_to_all | solution.py:11
  182.1 56.3 %all-gather.7.cloned.1.call-done = bf16[4096,2560]{1,0:T(8,128)(2,1)} async-done(((bf16[512,2560]{1,0:T(8,128)(2,1)}), bf16[4096,2560]{1,0:T(8,128)(2,1)}) %all-gather.7.cloned.1.call-update) | async-done | bytes 20971536 | tf_op jit(solution)/shard_map/all_gather | solution.py:14
  238.4 0.0 copy-done
  238.4 17.7 %fusion = (f32[2560]{0:T(1024)S(1)}, bf16[512,2560]{1,0:T(8,128)(2,1)}) fusion(f32[512]{0:T(512)S(1)} %copy-done, bf16[4096,512]{1,0:T(8,128)(2,1)} %bitcast.7, bf16[4096,2560]{1,0:T(8,128)(2,1)} %all-gather.7.cloned.1.call-done), kind=kOutput, calls=%fused_computation.1 | convolution fusion | flops 10743969792 | bytes 27799552 | tf_op jit(solution)/shard_map/dot_general | solution.py:12
  256.1 9.2 %all-gather.1 = f32[8,1,2560]{2,1,0:T(1,128)S(1)} all-gather(f32[1,1,2560]{2,1,0:T(1,128)S(1)} %reshape.9), channel_id=2, replica_groups=mesh['band'=8,'grid'=4] {'band'}, dimensions={0}, use_global_device_ids=true | all-gather | bytes 92160 | tf_op jit(solution)/shard_map/all_gather | solution.py:21
  265.3 0.1 reduce_sum.19
  265.4 0.6 broadcast_multiply_fusion
  (1 shorter events, 0.0 us)
Async XLA Ops:
  7.2 86.4 %all-gather.5.cloned.1.call-start = ((), (), s32[]{:S(2)}) async-start(), calls=%async_computation.1 | async-start | bytes 5242880 | tf_op jit(solution)/shard_map/all_gather | solution.py:10
  9.5 228.9 %all-gather.7.cloned.1.call-start = ((), (), s32[]{:S(2)}) async-start(), calls=%async_computation.2 | async-start | bytes 23592960 | tf_op jit(solution)/shard_map/all_gather | solution.py:14
  175.3 63.1 %copy-start = (f32[512]{0:T(512)S(1)}, f32[512]{0:T(512)}, u32[]{:S(2)}) copy-start(f32[512]{0:T(512)} %param.5) | copy-start | bytes 6148
Sparse Core Ops, SparseCore 0:
  10.1 83.4 all-gather.4
  95.5 142.8 all-gather.6
